TPU v7x, 128 devices: a whole 4x4x4 slice. The times are simulated.
128 devices in a mesh: dp: 64 (over z, y, x), tensor: 2 (over core).
Axes of the slice: x: 4, y: 4, z: 4, core: 2. Of those that a mesh axis runs over, the one named last changes fastest.
Arguments:
- current: float32 [128, 4096], P('dp'), may hold values from -6 to 6
- noise_draw: float32 [128, 4096], P('dp'), may hold values from -6 to 6
- labels: bfloat16 [128, 1152], P('dp'), may hold values from -6 to 6
- time_now: float32 [128], P('dp'), may hold values from 0.4 to 1
- step_size: float32 [128], P('dp'), may hold values from 0.005 to 0.02
- accept: int32 [128], P('dp'), may hold values 0 or 1
- patch_weight: bfloat16 [16, 1152], replicated, may hold values from -1.5 to 1.5
- time_in: bfloat16 [256, 1152], replicated, may hold values from -0.375 to 0.375
- time_out: bfloat16 [1152, 1152], replicated, may hold values from -0.1875 to 0.1875
- qkv_weight: bfloat16 [1, 1152, 3, 1152], P(None, None, None, 'tensor'), may hold values from -1 to 1
- out_weight: bfloat16 [1, 1152, 1152], P(None, None, 'tensor'), may hold values from -0.1875 to 0.1875
- ada_weight: bfloat16 [1, 1152, 3456], P(None, 'dp', 'tensor'), may hold values from -0.1875 to 0.1875
- final_ada: bfloat16 [1152, 2304], P('dp', 'tensor'), may hold values from -0.1875 to 0.1875
- final_proj: bfloat16 [1152, 16], replicated, may hold values from -0.1875 to 0.1875
Outputs:
- next_state: float32 [128, 4096], P('dp')
- error_norm: float32 [128], P('dp')
All inputs are finite; a program needn't handle non-finite values. No bound on the sum of `accept` on one device may be relied on, other than what follows from the above.
Results may differ from a plain program's by a relative error of at most 0.015.
Values may be sent and summed in bfloat16 or wider, within the bound.
A program may use at most 128 MiB of HBM per device.

v0:
```python
import math
import jax
import jax.numpy as jnp
from jax import lax
from jax.sharding import PartitionSpec as P

D = 1152
PATCH_VALS = 16
HEAD_DIM = 72
beta_low = 0.1
beta_high = 20.0
tol_abs = 0.0078
tol_rel = 0.05
norm_eps = 1e-06


def from_everyone(array, axis):
    peers = lax.axis_size(axis)
    return lax.all_to_all(
        jnp.broadcast_to(array[None], (peers, *array.shape)), axis, 0, 0, tiled=True
    )


def of_everyone(array, axis):
    return from_everyone(array, axis).astype(jnp.float32).sum(axis=0)


def beta_at(moments):
    return beta_low + (beta_high - beta_low) * moments


def sigma_at(moments):
    integral = beta_low * moments + 0.5 * (beta_high - beta_low) * moments * moments
    return jnp.sqrt(1.0 - jnp.exp(-integral))


def time_features(moments, feature_count):
    half_count = feature_count // 2
    freq_index = jnp.arange(half_count, dtype=jnp.float32)
    freq_rates = jnp.exp(-math.log(10000.0) * freq_index / half_count)
    angles = 1000.0 * moments[:, None] * freq_rates[None, :]
    return jnp.concatenate([jnp.cos(angles), jnp.sin(angles)], axis=1)


def position_table(positions, feature_count):
    half_count = feature_count // 2
    freq_index = jnp.arange(half_count, dtype=jnp.float32)
    freq_rates = jnp.exp(-math.log(10000.0) * freq_index / half_count)
    angles = positions.astype(jnp.float32)[:, None] * freq_rates[None, :]
    return jnp.concatenate([jnp.sin(angles), jnp.cos(angles)], axis=1)


def condition(moments, labels, time_in, time_out):
    features = time_features(moments, time_in.shape[0]).astype(jnp.bfloat16)
    hidden = jax.nn.silu(jnp.dot(features, time_in, preferred_element_type=jnp.float32)).astype(
        jnp.bfloat16
    )
    joined = labels.astype(jnp.float32) + jnp.dot(
        hidden, time_out, preferred_element_type=jnp.float32
    )
    return jax.nn.silu(joined).astype(jnp.bfloat16)


def layer_norm(values):
    average = jnp.mean(values, axis=-1, keepdims=True)
    centred = values - average
    spread_sq = jnp.mean(centred * centred, axis=-1, keepdims=True)
    return centred * lax.rsqrt(spread_sq + norm_eps)


def modulate(values, shift_vec, scale_vec):
    return (layer_norm(values) * (1.0 + scale_vec[:, None]) + shift_vec[:, None]).astype(
        jnp.bfloat16
    )


def drift(values, moments, noise_guess):
    beta_rate = beta_at(moments)[:, None]
    return 0.5 * beta_rate * values - beta_rate * noise_guess / sigma_at(moments)[:, None]


def attend(projected, head_dim):
    lat_count, token_count, _, feature_width = projected.shape
    head_count = feature_width // head_dim
    shaped = projected.reshape(lat_count, token_count, 3, head_count, head_dim)
    scores = jnp.einsum(
        "lqhe,lkhe->lhqk", shaped[:, :, 0], shaped[:, :, 1], preferred_element_type=jnp.float32
    ) * head_dim ** (-0.5)
    attn_probs = jax.nn.softmax(scores, axis=-1).astype(jnp.bfloat16)
    mixture = jnp.einsum(
        "lhqk,lkhe->lqhe", attn_probs, shaped[:, :, 2], preferred_element_type=jnp.float32
    )
    return mixture.astype(jnp.bfloat16).reshape(lat_count, token_count, feature_width)


def shards(
    current,
    noise_draw,
    labels,
    time_now,
    step_size,
    accept,
    patch_weight,
    time_in,
    time_out,
    qkv_weight,
    out_weight,
    ada_weight,
    final_ada,
    final_proj,
):
    lat_count = current.shape[0]
    tok_count = current.shape[1] // PATCH_VALS
    layer_total = ada_weight.shape[0]
    layer_cols = ada_weight.shape[2]
    final_cols = final_ada.shape[1]
    tensor_size = lax.axis_size("tensor")
    later_time = time_now - step_size
    moments = jnp.concatenate([time_now, later_time])
    cond_act = condition(moments, jnp.concatenate([labels, labels], axis=0), time_in, time_out)
    own_rows = ada_weight.shape[1]
    packed = jnp.concatenate(
        [ada_weight.transpose(1, 0, 2).reshape(own_rows, layer_total * layer_cols), final_ada],
        axis=1,
    )
    row_total = cond_act.shape[0]
    packed_width = packed.shape[1]
    mod_local = jnp.dot(
        cond_act,
        lax.all_gather(packed, "dp", axis=0, tiled=True),
        preferred_element_type=jnp.float32,
    )
    gathered = lax.all_gather(mod_local.astype(jnp.bfloat16), "tensor", axis=1, tiled=True).astype(
        mod_local.dtype
    )
    arranged = gathered.reshape(row_total, tensor_size, packed_width)
    layer_mods = arranged[:, :, : layer_total * layer_cols].reshape(
        row_total, tensor_size, layer_total, layer_cols
    )
    layer_mods = layer_mods.transpose(0, 2, 1, 3).reshape(
        row_total, layer_total, tensor_size * layer_cols
    )
    final_mods = arranged[:, :, layer_total * layer_cols :].reshape(
        row_total, tensor_size * final_cols
    )
    positions = position_table(jnp.arange(tok_count, dtype=jnp.int32), D)

    def evaluate(latents, mod_rows, final_rows):
        tokens = latents.reshape(lat_count, tok_count, PATCH_VALS).astype(jnp.bfloat16)
        stream = (
            jnp.einsum("ltc,cd->ltd", tokens, patch_weight, preferred_element_type=jnp.float32)
            + positions[None]
        )
        shift_attn, scale_attn, gate_attn = jnp.split(mod_rows[:, 0], 3, axis=1)
        attn_in = modulate(stream, shift_attn, scale_attn)
        projected = jnp.einsum(
            "ltd,dck->ltck", attn_in, qkv_weight[0], preferred_element_type=jnp.float32
        ).astype(jnp.bfloat16)
        attended = attend(projected, HEAD_DIM)
        partial_value = jnp.einsum(
            "ltk,dk->ltd", attended, out_weight[0], preferred_element_type=jnp.float32
        )
        attn_sum = of_everyone(partial_value.astype(jnp.bfloat16), "tensor").astype(jnp.float32)
        stream = stream + gate_attn[:, None] * attn_sum
        shift_final, scale_final = jnp.split(final_rows, 2, axis=1)
        final_in = modulate(stream, shift_final, scale_final)
        guessed = jnp.einsum(
            "ltd,dc->ltc", final_in, final_proj, preferred_element_type=jnp.float32
        )
        return guessed.reshape(lat_count, tok_count * PATCH_VALS)

    noise_now = evaluate(current, layer_mods[:lat_count], final_mods[:lat_count])
    drift_now = drift(current, time_now, noise_now)
    spread = jnp.sqrt(step_size * beta_at(time_now))[:, None] * noise_draw
    euler_state = current + step_size[:, None] * drift_now + spread
    noise_later = evaluate(euler_state, layer_mods[lat_count:], final_mods[lat_count:])
    drift_later = drift(euler_state, later_time, noise_later)
    heun_state = current + 0.5 * step_size[:, None] * (drift_now + drift_later) + spread
    scale_ref = jnp.maximum(tol_abs, tol_rel * jnp.maximum(jnp.abs(heun_state), jnp.abs(current)))
    scaled_gap = (euler_state - heun_state) / scale_ref
    error_norm = jnp.sqrt(jnp.sum(scaled_gap * scaled_gap, axis=1) / current.shape[1])
    next_state = jnp.where(accept[:, None] == 1, heun_state, current)
    return (next_state, error_norm)


def solution(mesh):
    in_specs = (
        P("dp", None),
        P("dp", None),
        P("dp", None),
        P("dp"),
        P("dp"),
        P("dp"),
        P(),
        P(),
        P(),
        P(None, None, None, "tensor"),
        P(None, None, "tensor"),
        P(None, "dp", "tensor"),
        P("dp", "tensor"),
        P(),
    )
    out_specs = (P("dp", None), P("dp"))
    return jax.shard_map(shards, mesh=mesh, in_specs=in_specs, out_specs=out_specs, check_vma=False)
```

profile of v0, /device:TPU:1, one launch (start us, length us, event | category | flops | bytes accessed | tf_op | source)
XLA Modules:
  0.0 162.8 jit_solution(1953090648457118049)
XLA Ops:
  7.2 0.0 copy-start
  7.2 0.0 all-gather.4.cloned.1.call-start
  7.2 1.8 %maximum_bitcast_fusion = bf16[1,18,2880]{2,1,0:T(8,128)(2,1)} fusion(bf16[18,1152]{1,0:T(8,128)(2,1)} %param.26, bf16[18,1728]{1,0:T(8,128)(2,1)} %bitcast.106), kind=kLoop, calls=%fused_computation.66 | loop fusion | flops 207360 | bytes 207360
  9.0 0.0 all-gather.4.cloned.1.call-update
  9.1 0.8 convert_element_type.83
  9.8 0.1 convert_element_type.84
  10.0 0.7 broadcast_multiply_fusion.4
  10.7 0.7 maximum_multiply_fusion
  11.4 2.3 %multiply_sine_fusion = (f32[256,576]{1,0:T(8,128)S(1)}, f32[256,576]{1,0:T(8,128)S(1)}) fusion(f32[576]{0:T(1024)S(1)} %multiply_exponential_fusion, f32[256]{0:T(256)S(1)} %iota_convert_fusion), kind=kLoop, calls=%fused_computation.57 | loop fusion | flops 147456 | bytes 1182976 | tf_op jit(solution)/shard_map/sin | solution.py:50
  13.8 0.2 pad_maximum_fusion
  14.1 1.0 copy-done.4
  15.1 0.5 fusion.78
  15.6 1.4 copy-done.2
  17.0 0.4 multiply_reduce_fusion.5
  17.4 0.1 fusion.58
  17.5 0.2 fusion.60
  17.7 76.3 %all-gather.4.cloned.1.call-done = bf16[64,18,2880]{2,1,0:T(8,128)(2,1)} async-done(((bf16[1,18,2880]{2,1,0:T(8,128)(2,1)}), bf16[64,18,2880]{2,1,0:T(8,128)(2,1)}) %all-gather.4.cloned.1.call-update) | async-done | bytes 6635536 | tf_op jit(solution)/shard_map/all_gather | solution.py:130
  94.0 10.0 %reshape.163 = bf16[1152,2880]{1,0:T(8,128)(2,1)} reshape(bf16[64,18,2880]{2,1,0:T(8,128)(2,1)} %all-gather.4.cloned.1.call-done) | data formatting | bytes 13271040
  104.1 4.3 %fusion.8 = bf16[1,2880,4]{1,2,0:T(4,128)(2,1)S(1)} fusion(bf16[1152,2880]{1,0:T(8,128)(2,1)} %reshape.163, bf16[1152,1152]{1,0:T(8,128)(2,1)S(1)} %copy-done, f32[4,1152]{1,0:T(4,128)S(1)} %fusion.60, bf16[2,1152]{1,0:T(2,128)(2,1)S(1)} %copy-done.9), kind=kOutput, calls=%fused_computation.19 | convolution fusion | flops 37239552 | bytes 9335808 | tf_op jit(solution)/shard_map/dot_general | solution.py:128
  108.4 2.3 %all-gather.1 = bf16[2,2880,4]{1,2,0:T(4,128)(2,1)S(1)} all-gather(bf16[1,2880,4]{1,2,0:T(4,128)(2,1)S(1)} %fusion.8), channel_id=1, replica_groups=mesh['dp'=64,'tensor'=2] {'tensor'}, dimensions={0}, use_global_device_ids=true | all-gather | bytes 69120 | tf_op jit(solution)/shard_map/all_gather | solution.py:133
  110.7 0.1 reshape.168
  110.9 0.1 reshape.161
  111.0 0.1 slice_bitcast_fusion.12
  111.1 0.1 squeeze.32
  111.3 5.6 %fusion.17 = bf16[2,256,3,576]{1,3,2,0:T(8,128)(2,1)S(1)} fusion(bf16[1,1152,3,576]{1,3,2,0:T(8,128)(2,1)} %param.23, f32[2,256,1152]{2,1,0:T(8,128)} %copy-done.2, f32[2,1152]{1,0:T(2,128)S(1)} %get-tuple-element.21, f32[2,1152]{1,0:T(2,128)S(1)} %get-tuple-element.22, f32[2,256]{1,0:T(2,128)S(1)} %add_rsqrt_fusion.3, ...), kind=kOutput, calls=%fused_computation.37 | convolution fusion | flops 2042265600 | bytes 8132608 | tf_op jit(solution)/shard_map/ltd,dck->ltck/dot_general | solution.py:156
  116.8 0.7 fusion.42
  117.6 3.2 %fusion.79 = (f32[2,8,256]{2,1,0:T(8,128)S(1)}, f32[2,8,256,256]{2,3,1,0:T(8,128)S(1)}) fusion(f32[2,8,256,256]{2,3,1,0:T(8,128)S(1)} %fusion.42), kind=kOutput, calls=%fused_computation.139 | output fusion | flops 4194559 | bytes 8404992 | tf_op jit(solution)/shard_map/sub | solution.py:89
  120.8 0.0 copy-start.11
  120.8 0.5 fusion.26
  121.4 0.8 copy-done.11
  122.2 1.2 convolution_convert_fusion.2
  123.4 0.2 broadcast_in_dim.10
  123.5 5.7 %all_to_all.10 = bf16[2,2,256,1152]{3,2,1,0:T(8,128)(2,1)S(1)} all-to-all(bf16[2,2,256,1152]{3,2,1,0:T(8,128)(2,1)S(1)} %broadcast_in_dim.10), channel_id=1, replica_groups=mesh['dp'=64,'tensor'=2] {'tensor'}, dimensions={0} | all-to-all | bytes 4718592 | tf_op jit(solution)/shard_map/all_to_all | solution.py:19
  129.2 0.4 convert_reduce_fusion.1
  129.6 1.3 copy-done.3
  130.9 0.3 fusion.74
  131.3 0.4 multiply_reduce_fusion.4
  131.6 0.0 copy-start.8
  131.6 0.0 copy-start.10
  131.7 0.3 copy-done.13
  132.0 0.6 fusion.39
  132.6 0.2 reshape.156
  132.8 0.1 fusion.73
  132.9 0.1 convert_element_type.99
  133.0 1.8 %fusion.80 = (f32[2,256]{1,0:T(2,128)S(1)}, f32[2,256,1152]{2,1,0:T(8,128)S(1)}) fusion(f32[256,1152]{1,0:T(8,128)} %copy-done.4, bf16[2,256,16]{2,1,0:T(8,128)(2,1)S(1)} %convert_element_type.99, bf16[16,1152]{1,0:T(8,128)(2,1)S(1)} %copy-done.7), kind=kOutput, calls=%fused_computation.140 | convolution fusion | flops 20053504 | bytes 3594240 | tf_op jit(solution)/shard_map/ltc,cd->ltd/dot_general | solution.py:151
  134.8 0.4 multiply_reduce_fusion.3
  135.2 0.1 squeeze.38
  135.4 4.8 %fusion.20 = bf16[2,256,3,576]{1,3,2,0:T(8,128)(2,1)S(1)} fusion(bf16[1,1152,3,576]{1,3,2,0:T(8,128)(2,1)} %param.23, f32[2,256,1152]{2,1,0:T(8,128)S(1)} %get-tuple-element.43, f32[2,1152]{1,0:T(2,128)S(1)} %get-tuple-element.18, f32[2,1152]{1,0:T(2,128)S(1)} %get-tuple-element.19, f32[2,256]{1,0:T(2,128)S(1)} %add_rsqrt_fusion.1, ...), kind=kOutput, calls=%fused_computation.38 | convolution fusion | flops 2042265600 | bytes 8132608 | tf_op jit(solution)/shard_map/ltd,dck->ltck/dot_general | solution.py:156
  140.2 0.7 fusion.41
  141.0 3.2 %fusion.81 = (f32[2,8,256]{2,1,0:T(8,128)S(1)}, f32[2,8,256,256]{2,3,1,0:T(8,128)S(1)}) fusion(f32[2,8,256,256]{2,3,1,0:T(8,128)S(1)} %fusion.41), kind=kOutput, calls=%fused_computation.141 | output fusion | flops 4194559 | bytes 8404992 | tf_op jit(solution)/shard_map/sub | solution.py:89
  144.2 0.0 copy-start.12
  144.2 0.5 fusion.25
  144.7 0.8 copy-done.12
  145.5 1.2 convolution_convert_fusion.1
  146.7 0.2 broadcast_in_dim.11
  146.9 5.6 %all_to_all.11 = bf16[2,2,256,1152]{3,2,1,0:T(8,128)(2,1)S(1)} all-to-all(bf16[2,2,256,1152]{3,2,1,0:T(8,128)(2,1)S(1)} %broadcast_in_dim.11), channel_id=1, replica_groups=mesh['dp'=64,'tensor'=2] {'tensor'}, dimensions={0} | all-to-all | bytes 4718592 | tf_op jit(solution)/shard_map/all_to_all | solution.py:19
  152.5 0.4 convert_reduce_fusion
  152.9 0.4 fusion.72
  153.3 0.4 multiply_reduce_fusion.2
  153.7 0.6 fusion.40
  154.3 0.2 reshape.159
  154.5 0.3 multiply_reduce_fusion.6
  154.8 0.5 multiply_sqrt_fusion
  155.3 0.7 broadcast_select_fusion
  (40 shorter events, 0.2 us)
Async XLA Ops:
  7.2 96.9 %copy-start = (bf16[1152,1152]{1,0:T(8,128)(2,1)S(1)}, bf16[1152,1152]{1,0:T(8,128)(2,1)}, u32[]{:S(2)}) copy-start(bf16[1152,1152]{1,0:T(8,128)(2,1)} %param.22) | copy-start | bytes 7962628
  7.2 7.9 %copy-start.7 = (bf16[16,1152]{1,0:T(8,128)(2,1)S(1)}, bf16[16,1152]{1,0:T(8,128)(2,1)}, u32[]{:S(2)}) copy-start(bf16[16,1152]{1,0:T(8,128)(2,1)} %param.20) | copy-start | bytes 110596
  7.2 86.8 %all-gather.4.cloned.1.call-start = ((), (), s32[]{:S(2)}) async-start(), calls=%async_computation.2 | async-start | bytes 9185280 | tf_op jit(solution)/shard_map/all_gather | solution.py:130
  14.0 1.0 copy-start.4
  15.1 2.3 %copy-start.14 = (s32[2]{0:T(128)S(1)}, s32[2]{0:T(128)}, u32[]{:S(2)}) copy-start(s32[2]{0:T(128)} %param.19) | copy-start | bytes 28
  15.1 2.5 %copy-start.5 = (bf16[256,1152]{1,0:T(8,128)(2,1)S(1)}, bf16[256,1152]{1,0:T(8,128)(2,1)}, u32[]{:S(2)}) copy-start(bf16[256,1152]{1,0:T(8,128)(2,1)} %param.21) | copy-start | bytes 1769476
  15.6 1.4 copy-start.2
  17.7 86.3 %copy-start.9 = (bf16[2,1152]{1,0:T(2,128)(2,1)S(1)}, bf16[2,1152]{1,0:T(2,128)(2,1)}, u32[]{:S(2)}) copy-start(bf16[2,1152]{1,0:T(2,128)(2,1)} %param.16) | copy-start | bytes 13828
  120.8 1.3 copy-start.11
  129.2 1.7 %copy-start.3 = (f32[2,256,1152]{2,1,0:T(8,128)S(1)}, f32[2,256,1152]{2,1,0:T(8,128)}, u32[]{:S(2)}) copy-start(f32[2,256,1152]{2,1,0:T(8,128)} %copy-done.2) | copy-start | bytes 7077892
  131.2 0.8 copy-start.13
  131.6 1.1 copy-start.6
  131.6 1.1 copy-start.8
  131.6 1.1 copy-start.10
  144.2 1.3 copy-start.12
  153.3 2.7 %copy-start.1 = (bf16[1152,1152]{1,0:T(8,128)(2,1)S(1)}, bf16[1152,1152]{1,0:T(8,128)(2,1)}, u32[]{:S(2)}) copy-start(bf16[1152,1152]{1,0:T(8,128)(2,1)} %param.22) | copy-start | bytes 7962628
Sparse Core Ops, SparseCore 0:
  10.9 83.1 all-gather.3
where the time goes:
time: 164 us; the launch traced here: 163 us
  waiting for transfers between devices  76.3 us (47%)
  matrix products  23.3 us (14%)
  other arithmetic  17.9 us (11%)
  local copies, waits for them, and re-layouts  17.2 us (10%)
  between operations  14.5 us (9%)
  blocking collectives  13.6 us (8%)
    all_gather x1, waiting for transfers between devices, shards(): lax.all_gather(packed, 'dp', axis=0, tiled=True)  76.3 us
    unnamed x34, local copies, waits for them, and re-layouts  15.8 us
    all_to_all x2, blocking collectives, from_everyone(): lax.all_to_all(jnp.broadcast_to(array[None], (peers, *array.shape)), axis...  11.2 us
    dot_general x2, matrix products, evaluate(): jnp.einsum('ltd,dck->ltck', attn_in, qkv_weight[0], preferred_element_typ...  10.4 us
    sub x2, other arithmetic, attend(): attn_probs = jax.nn.softmax(scores, axis=-1).astype(jnp.bfloat16)  6.48 us
    dot_general x1, matrix products, shards(): jnp.dot(cond_act, lax.all_gather(packed, 'dp', axis=0, tiled=True), prefe...  4.3 us
  transfers between devices with their start and end apart: 1, of which 1 were waited for; matrix products, arithmetic and copies ran while one was open for 4% of the time, Pallas kernels for 0%

commit v1 on v0

--- a/solution.py
+++ b/solution.py
@@ -12,6 +12,17 @@
 tol_abs = 0.0078
 tol_rel = 0.05
 norm_eps = 1e-06
+
+
+def bring_ticks_over_axis(matrix, k_dim):
+    p_count = lax.psum(1, "dp")
+    return lax.all_to_all(
+        jnp.tile(matrix, [p_count if k0 == k_dim else 1 for k0 in range(matrix.ndim)]),
+        "dp",
+        split_axis=k_dim,
+        concat_axis=k_dim,
+        tiled=True,
+    )
 
 
 def from_everyone(array, axis):
@@ -126,9 +137,7 @@
     row_total = cond_act.shape[0]
     packed_width = packed.shape[1]
     mod_local = jnp.dot(
-        cond_act,
-        lax.all_gather(packed, "dp", axis=0, tiled=True),
-        preferred_element_type=jnp.float32,
+        cond_act, bring_ticks_over_axis(packed, 0), preferred_element_type=jnp.float32
     )
     gathered = lax.all_gather(mod_local.astype(jnp.bfloat16), "tensor", axis=1, tiled=True).astype(
         mod_local.dtype

time: 164 us -> 225 us (1.37)
  the two profiles are of different devices: /device:TPU:1 before, /device:TPU:5 now
where the time goes in v1:
time: 225 us; the launch traced here: 224 us
  waiting for transfers between devices  137 us (61%)
  matrix products  23.3 us (10%)
  local copies, waits for them, and re-layouts  21.4 us (10%)
  other arithmetic  15.2 us (7%)
  blocking collectives  14.5 us (6%)
  starting transfers between devices  11.2 us (5%)
    all_to_all x1, waiting for transfers between devices, bring_ticks_over_axis(): lax.all_to_all(jnp.tile(matrix, [p_count if k0 == k_dim else 1 for k0 in...  137 us
    all_to_all x2, blocking collectives, from_everyone(): lax.all_to_all(jnp.broadcast_to(array[None], (peers, *array.shape)), axis...  11.2 us
    all_to_all x1, starting transfers between devices, bring_ticks_over_axis(): lax.all_to_all(jnp.tile(matrix, [p_count if k0 == k_dim else 1 for k0 in...  11.2 us
    dot_general x2, matrix products, evaluate(): jnp.einsum('ltd,dck->ltck', attn_in, qkv_weight[0], preferred_element_typ...  10.4 us
    all_to_all x1, local copies, waits for them, and re-layouts, bring_ticks_over_axis(): lax.all_to_all(jnp.tile(matrix, [p_count if k0 == k_dim else 1 for k0 in...  10 us
    sub x2, other arithmetic, attend(): attn_probs = jax.nn.softmax(scores, axis=-1).astype(jnp.bfloat16)  6.48 us
    unnamed x35, local copies, waits for them, and re-layouts  5.79 us
  transfers between devices with their start and end apart: 1, of which 1 were waited for; matrix products, arithmetic and copies ran while one was open for 2% of the time, Pallas kernels for 0%

profile of v1, /device:TPU:5, one launch (start us, length us, event | category | flops | bytes accessed | tf_op | source)
XLA Modules:
  0.0 224.0 jit_solution(1841972504329356452)
XLA Ops:
  0.6 0.0 copy-start
  0.6 1.2 pad_maximum_fusion.1
  1.8 4.1 %tile.2 = bf16[64,18,2880]{2,1,0:T(8,128)(2,1)} broadcast(bf16[18,2880]{1,0:T(8,128)(2,1)S(1)} %pad_maximum_fusion.1), dimensions={1,2} | broadcast | bytes 6739200 | tf_op jit(solution)/shard_map/tile | solution.py:20
  5.9 11.2 %all-to-all-start = ((bf16[64,18,2880]{2,1,0:T(8,128)(2,1)}), bf16[64,18,2880]{2,1,0:T(8,128)(2,1)}, u32[]{:S(2)}, u32[]{:S(2)}) async-start(bf16[64,18,2880]{2,1,0:T(8,128)(2,1)} %tile.2), calls=%async_computation | async-start | bytes 18087936 | tf_op jit(solution)/shard_map/all_to_all | solution.py:19
  17.1 0.0 copy-start.7
  17.2 0.1 convert_element_type.84
  17.3 0.0 copy-done.10
  17.3 0.0 copy-done.11
  17.4 0.1 maximum_multiply_fusion
  17.5 2.3 %multiply_sine_fusion = (f32[256,576]{1,0:T(8,128)S(1)}, f32[256,576]{1,0:T(8,128)S(1)}) fusion(f32[576]{0:T(1024)S(1)} %multiply_exponential_fusion, f32[256]{0:T(256)S(1)} %iota_convert_fusion), kind=kLoop, calls=%fused_computation.57 | loop fusion | flops 147456 | bytes 1182976 | tf_op jit(solution)/shard_map/sin | solution.py:61
  19.8 0.2 pad_maximum_fusion
  20.1 1.0 copy-done.4
  21.1 0.5 fusion.78
  21.7 1.4 copy-done.2
  23.0 0.4 multiply_reduce_fusion.5
  23.4 0.1 fusion.58
  23.6 0.2 fusion.60
  23.8 137.3 %all-to-all-done = bf16[64,18,2880]{2,1,0:T(8,128)(2,1)} async-done(((bf16[64,18,2880]{2,1,0:T(8,128)(2,1)}), bf16[64,18,2880]{2,1,0:T(8,128)(2,1)}, u32[]{:S(2)}, u32[]{:S(2)}) %all-to-all-start) | async-done | bytes 6635552 | tf_op jit(solution)/shard_map/all_to_all | solution.py:19
  161.1 10.0 %all_to_all.13 = bf16[1152,2880]{1,0:T(8,128)(2,1)} reshape(bf16[64,18,2880]{2,1,0:T(8,128)(2,1)} %all-to-all-done) | data formatting | bytes 13271040 | tf_op jit(solution)/shard_map/all_to_all | solution.py:19
  171.1 4.3 %fusion.8 = bf16[1,2880,4]{1,2,0:T(4,128)(2,1)S(1)} fusion(bf16[1152,2880]{1,0:T(8,128)(2,1)} %all_to_all.13, bf16[1152,1152]{1,0:T(8,128)(2,1)S(1)} %copy-done, f32[4,1152]{1,0:T(4,128)S(1)} %fusion.60, bf16[2,1152]{1,0:T(2,128)(2,1)S(1)} %copy-done.9), kind=kOutput, calls=%fused_computation.19 | convolution fusion | flops 37239552 | bytes 9335808 | tf_op jit(solution)/shard_map/dot_general | solution.py:139
  175.4 3.2 %all-gather = bf16[2,2880,4]{1,2,0:T(4,128)(2,1)S(1)} all-gather(bf16[1,2880,4]{1,2,0:T(4,128)(2,1)S(1)} %fusion.8), channel_id=1, replica_groups=mesh['dp'=64,'tensor'=2] {'tensor'}, dimensions={0}, use_global_device_ids=true | all-gather | bytes 69120 | tf_op jit(solution)/shard_map/all_gather | solution.py:142
  178.7 0.1 reshape.173
  178.8 0.1 reshape.168
  179.0 0.1 slice_bitcast_fusion.12
  179.1 0.1 squeeze.32
  179.2 5.6 %fusion.17 = bf16[2,256,3,576]{1,3,2,0:T(8,128)(2,1)S(1)} fusion(bf16[1,1152,3,576]{1,3,2,0:T(8,128)(2,1)} %param.23, f32[2,256,1152]{2,1,0:T(8,128)} %copy-done.2, f32[2,1152]{1,0:T(2,128)S(1)} %get-tuple-element.21, f32[2,1152]{1,0:T(2,128)S(1)} %get-tuple-element.22, f32[2,256]{1,0:T(2,128)S(1)} %add_rsqrt_fusion.3, ...), kind=kOutput, calls=%fused_computation.37 | convolution fusion | flops 2042265600 | bytes 8132608 | tf_op jit(solution)/shard_map/ltd,dck->ltck/dot_general | solution.py:165
  184.8 0.8 fusion.42
  185.5 3.2 %fusion.79 = (f32[2,8,256]{2,1,0:T(8,128)S(1)}, f32[2,8,256,256]{2,3,1,0:T(8,128)S(1)}) fusion(f32[2,8,256,256]{2,3,1,0:T(8,128)S(1)} %fusion.42), kind=kOutput, calls=%fused_computation.139 | output fusion | flops 4194559 | bytes 8404992 | tf_op jit(solution)/shard_map/sub | solution.py:100
  188.8 0.0 copy-start.12
  188.8 0.5 fusion.26
  189.3 0.8 copy-done.12
  190.1 1.2 convolution_convert_fusion.2
  191.3 0.2 broadcast_in_dim.10
  191.5 5.7 %all_to_all.19 = bf16[2,2,256,1152]{3,2,1,0:T(8,128)(2,1)S(1)} all-to-all(bf16[2,2,256,1152]{3,2,1,0:T(8,128)(2,1)S(1)} %broadcast_in_dim.10), channel_id=1, replica_groups=mesh['dp'=64,'tensor'=2] {'tensor'}, dimensions={0} | all-to-all | bytes 4718592 | tf_op jit(solution)/shard_map/all_to_all | solution.py:30
  197.2 0.4 convert_reduce_fusion.1
  197.6 1.3 copy-done.3
  198.9 0.4 fusion.74
  199.3 0.4 multiply_reduce_fusion.4
  199.7 0.3 copy-done.14
  200.0 0.6 fusion.39
  200.6 0.2 reshape.163
  200.8 0.1 fusion.73
  200.9 0.1 convert_element_type.99
  201.1 1.8 fusion.80
  202.9 0.4 multiply_reduce_fusion.3
  203.3 0.1 squeeze.38
  203.4 4.8 %fusion.20 = bf16[2,256,3,576]{1,3,2,0:T(8,128)(2,1)S(1)} fusion(bf16[1,1152,3,576]{1,3,2,0:T(8,128)(2,1)} %param.23, f32[2,256,1152]{2,1,0:T(8,128)S(1)} %get-tuple-element.43, f32[2,1152]{1,0:T(2,128)S(1)} %get-tuple-element.18, f32[2,1152]{1,0:T(2,128)S(1)} %get-tuple-element.19, f32[2,256]{1,0:T(2,128)S(1)} %add_rsqrt_fusion.1, ...), kind=kOutput, calls=%fused_computation.38 | convolution fusion | flops 2042265600 | bytes 8132608 | tf_op jit(solution)/shard_map/ltd,dck->ltck/dot_general | solution.py:165
  208.3 0.7 fusion.41
  209.0 3.2 %fusion.81 = (f32[2,8,256]{2,1,0:T(8,128)S(1)}, f32[2,8,256,256]{2,3,1,0:T(8,128)S(1)}) fusion(f32[2,8,256,256]{2,3,1,0:T(8,128)S(1)} %fusion.41), kind=kOutput, calls=%fused_computation.141 | output fusion | flops 4194559 | bytes 8404992 | tf_op jit(solution)/shard_map/sub | solution.py:100
  212.3 0.0 copy-start.13
  212.3 0.5 fusion.25
  212.8 0.8 copy-done.13
  213.6 1.2 convolution_convert_fusion.1
  214.8 0.2 broadcast_in_dim.11
  215.0 5.5 %all_to_all.20 = bf16[2,2,256,1152]{3,2,1,0:T(8,128)(2,1)S(1)} all-to-all(bf16[2,2,256,1152]{3,2,1,0:T(8,128)(2,1)S(1)} %broadcast_in_dim.11), channel_id=1, replica_groups=mesh['dp'=64,'tensor'=2] {'tensor'}, dimensions={0} | all-to-all | bytes 4718592 | tf_op jit(solution)/shard_map/all_to_all | solution.py:30
  220.5 0.4 convert_reduce_fusion
  220.9 0.4 fusion.72
  221.3 0.0 copy-start.1
  221.3 0.4 multiply_reduce_fusion.2
  221.7 0.6 fusion.40
  222.3 0.2 reshape.166
  222.5 0.3 multiply_reduce_fusion.6
  222.8 0.5 multiply_sqrt_fusion
  223.3 0.7 broadcast_select_fusion
  (42 shorter events, 0.3 us)
Async XLA Ops:
  0.6 170.5 %copy-start = (bf16[1152,1152]{1,0:T(8,128)(2,1)S(1)}, bf16[1152,1152]{1,0:T(8,128)(2,1)}, u32[]{:S(2)}) copy-start(bf16[1152,1152]{1,0:T(8,128)(2,1)} %param.22) | copy-start | bytes 7962628
  5.9 11.2 %copy-start.6 = (f32[2,4096]{1,0:T(2,128)S(1)}, f32[2,4096]{1,0:T(2,128)}, u32[]{:S(2)}) copy-start(f32[2,4096]{1,0:T(2,128)} %param.14) | copy-start | bytes 98308
  5.9 11.4 %copy-start.10 = (f32[2]{0:T(128)S(1)}, f32[2]{0:T(128)}, u32[]{:S(2)}) copy-start(f32[2]{0:T(128)} %param.18) | copy-start | bytes 28
  5.9 11.4 %copy-start.11 = (f32[2]{0:T(128)S(1)}, f32[2]{0:T(128)}, u32[]{:S(2)}) copy-start(f32[2]{0:T(128)} %param.17) | copy-start | bytes 28
  5.9 155.2 %all-to-all-start = ((bf16[64,18,2880]{2,1,0:T(8,128)(2,1)}), bf16[64,18,2880]{2,1,0:T(8,128)(2,1)}, u32[]{:S(2)}, u32[]{:S(2)}) async-start(bf16[64,18,2880]{2,1,0:T(8,128)(2,1)} %tile.2), calls=%async_computation | async-start | bytes 18087936 | tf_op jit(solution)/shard_map/all_to_all | solution.py:19
  17.1 4.0 %copy-start.7 = (bf16[16,1152]{1,0:T(8,128)(2,1)S(1)}, bf16[16,1152]{1,0:T(8,128)(2,1)}, u32[]{:S(2)}) copy-start(bf16[16,1152]{1,0:T(8,128)(2,1)} %param.20) | copy-start | bytes 110596
  20.1 1.0 copy-start.4
  21.1 2.3 %copy-start.15 = (s32[2]{0:T(128)S(1)}, s32[2]{0:T(128)}, u32[]{:S(2)}) copy-start(s32[2]{0:T(128)} %param.19) | copy-start | bytes 28
  21.1 2.5 %copy-start.5 = (bf16[256,1152]{1,0:T(8,128)(2,1)S(1)}, bf16[256,1152]{1,0:T(8,128)(2,1)}, u32[]{:S(2)}) copy-start(bf16[256,1152]{1,0:T(8,128)(2,1)} %param.21) | copy-start | bytes 1769476
  21.6 1.4 copy-start.2
  23.8 147.3 %copy-start.9 = (bf16[2,1152]{1,0:T(2,128)(2,1)S(1)}, bf16[2,1152]{1,0:T(2,128)(2,1)}, u32[]{:S(2)}) copy-start(bf16[2,1152]{1,0:T(2,128)(2,1)} %param.16) | copy-start | bytes 13828
  188.8 1.3 copy-start.12
  197.2 1.7 copy-start.3
  199.3 0.8 copy-start.14
  199.7 1.1 copy-start.8
  212.3 1.3 copy-start.13
  221.3 2.7 %copy-start.1 = (bf16[1152,1152]{1,0:T(8,128)(2,1)S(1)}, bf16[1152,1152]{1,0:T(8,128)(2,1)}, u32[]{:S(2)}) copy-start(bf16[1152,1152]{1,0:T(8,128)(2,1)} %param.22) | copy-start | bytes 7962628
